TPU v7x, 32 devices: a whole 2x2x4 slice. The times are simulated.
32 devices in a mesh: ta: 2 (over core), gx: 16 (over z, y, x).
Axes of the slice: x: 2, y: 2, z: 4, core: 2. Of those that a mesh axis runs over, the one named last changes fastest.
Arguments:
- time_links: float32 [6, 2, 3, 3, 96, 4608], P('ta', None, None, None, 'gx'), may hold values from -1 to 1, as said below
Outputs:
- loop_planes: float32 [96, 2, 4608], P('gx', None, 'ta')
- correlator: float32 [96, 49], P('gx')
Inputs may be any that keep to these rules, and one draw needn't show every extreme that they name: At every site and time, the matrix time_links[t, 0] + i time_links[t, 1] is special unitary.
All inputs are finite; a program needn't handle non-finite values.
Results may differ from a plain program's by a relative error of at most 0.00029.
Values sent between devices are 32-bit elements; how exact they have to be, the bound alone decides.
A program may use at most 64 MiB of HBM per device.

v0:
```python
import jax
import jax.numpy as jnp
from jax import lax
from jax.sharding import PartitionSpec as P


def prefix(value, axis, join, neutral):
    count, mine = (lax.axis_size(axis), lax.axis_index(axis))
    pieces = lax.all_gather(value, axis)
    subtotal = jnp.full_like(value, 0) + jnp.asarray(neutral, value.dtype)

    def step(position, subtotal):
        longer = join(subtotal, pieces[position])
        return jnp.where(position < mine, longer, subtotal)

    return lax.fori_loop(0, count - 1, step, subtotal)


def spread(value, axis, source):
    kept = jnp.where(lax.axis_index(axis) == source, value, 0).astype(value.dtype)
    return lax.psum(kept, axis)


def complex_mul(left, right):
    terms_real = []
    terms_imag = []
    for middle in range(3):
        left_real = left[0][:, middle : middle + 1]
        left_imag = left[1][:, middle : middle + 1]
        right_real = right[0][middle : middle + 1]
        right_imag = right[1][middle : middle + 1]
        terms_real.append(left_real * right_real - left_imag * right_imag)
        terms_imag.append(left_real * right_imag + left_imag * right_real)
    return jnp.stack(
        [
            terms_real[0] + terms_real[1] + terms_real[2],
            terms_imag[0] + terms_imag[1] + terms_imag[2],
        ]
    )


def trace_third(matrix):
    return (matrix[:, 0, 0] + matrix[:, 1, 1] + matrix[:, 2, 2]) / 3.0


def correlation(own_rows, others):
    return lax.dot_general(
        own_rows,
        others,
        (((1,), (1,)), ((), ())),
        precision=lax.Precision.HIGHEST,
        preferred_element_type=jnp.float32,
    )


def by_separation(products, offset, longest, period):
    row_index = lax.broadcasted_iota(jnp.int32, products.shape, 0)
    column_index = lax.broadcasted_iota(jnp.int32, products.shape, 1)
    separation = offset + column_index - row_index
    separation = separation % period
    targets = jnp.arange(longest + 1, dtype=jnp.int32)
    selector = (separation[:, :, None] == targets).astype(jnp.float32)
    return jnp.sum(products[:, :, None] * selector, axis=1)


def per_device(time_links):
    local_product = time_links[0]
    for slice_index in range(1, time_links.shape[0]):
        local_product = complex_mul(local_product, time_links[slice_index])
    plane_sites = time_links.shape[-1]
    ta_count = lax.axis_size("ta")
    site_share = plane_sites // ta_count
    unit_matrix = jnp.broadcast_to(
        jnp.eye(3, dtype=jnp.float32)[:, :, None, None], local_product.shape[1:]
    )
    identity = jnp.stack([unit_matrix, jnp.zeros_like(unit_matrix)])
    earlier = prefix(local_product, "ta", complex_mul, identity)
    full_product = complex_mul(earlier, local_product)
    traces = spread(trace_third(full_product), "ta", ta_count - 1)
    own_share = lax.dynamic_slice_in_dim(traces, lax.axis_index("ta") * site_share, site_share, 2)
    loop_planes = jnp.transpose(own_share, (1, 0, 2))
    planes = loop_planes.shape[0]
    flat_width = loop_planes.shape[1] * loop_planes.shape[2]
    gx_count = lax.axis_size("gx")
    far_blocks = gx_count // 2
    longest = planes * far_blocks
    own_rows = loop_planes.reshape(planes, flat_width)
    shard_rows = lax.all_gather(loop_planes, "gx", axis=0, tiled=True)
    products = correlation(own_rows, shard_rows.reshape(shard_rows.shape[0], flat_width))
    totals_part = by_separation(
        products, -lax.axis_index("gx") * planes, longest, planes * gx_count
    )
    correlator = lax.psum(totals_part, "ta") / plane_sites
    return (loop_planes, correlator)


def solution(mesh):
    in_specs = (P("ta", None, None, None, "gx", None),)
    out_specs = (P("gx", None, "ta"), P("gx", None))
    return jax.shard_map(
        per_device, mesh=mesh, in_specs=in_specs, out_specs=out_specs, check_vma=False
    )
```

profile of v0, /device:TPU:0, one launch (start us, length us, event | category | flops | bytes accessed | tf_op | source)
XLA Modules:
  0.0 143.7 jit_solution(14677089066934302279)
XLA Ops:
  7.2 5.7 %fusion.13 = (f32[1,1,1,3,6,4608]{5,1,4,3,2,0:T(1,128)S(1)}, f32[1,1,1,3,6,4608]{5,1,4,3,2,0:T(1,128)S(1)}, f32[1,1,1,3,6,4608]{5,1,4,3,2,0:T(1,128)S(1)}, f32[1...) fusion(f32[3,2,3,3,6,4608]{5,1,4,3,2,0:T(2,128)} %param.1), kind=kLoop, calls=%fused_computation.88 | loop fusion | bytes 7962624 | tf_op jit(solution)/shard_map/slice | solution.py:30
  12.9 3.9 %fusion.14 = (f32[1,1,3,3,6,4608]{5,1,4,3,2,0:T(1,128)S(1)}, f32[1,1,3,3,6,4608]{5,1,4,3,2,0:T(1,128)S(1)}) fusion(f32[3,2,3,3,6,4608]{5,1,4,3,2,0:T(2,128)} %param.1), kind=kLoop, calls=%fused_computation.89 | loop fusion | bytes 3981312 | tf_op jit(solution)/shard_map/slice | solution.py:28
  16.9 0.3 copy_bitcast_fusion
  17.4 0.1 copy_bitcast_fusion.8
  17.5 0.1 copy_bitcast_fusion.10
  17.8 1.0 subtract_add_fusion.4
  19.3 0.3 copy-done.1
  19.7 0.1 copy-done.2
  19.8 0.1 copy-done.3
  19.9 0.2 copy-done.4
  20.1 0.9 subtract_add_fusion.3
  21.0 1.8 %pad_maximum_fusion = f32[2,3,3,6,4608]{4,3,2,1,0:T(8,128)} fusion(f32[1,3,3,6,4608]{4,3,2,1,0:T(8,128)S(1)} %get-tuple-element.56, f32[1,3,3,6,4608]{4,3,2,1,0:T(8,128)S(1)} %get-tuple-element.55), kind=kLoop, calls=%fused_computation | loop fusion | flops 497664 | bytes 3981312 | tf_op jit(solution)/shard_map/stack | solution.py:34
  22.8 0.2 all-reduce.3.cloned.1.call-start
  23.1 2.4 %subtract_add_fusion.1 = (f32[3,3,6,4608]{3,2,1,0:T(8,128)S(1)}, f32[3,3,6,4608]{3,2,1,0:T(8,128)S(1)}) fusion(f32[3,6,4608]{2,1,0:T(8,128)S(1)} %get-tuple-element.90, f32[3,6,4608]{2,1,0:T(8,128)S(1)} %get-tuple-element.77, f32[3,6,4608]{2,1,0:T(8,128)S(1)} %get-tuple-element.91, f32[3,6,4608]{2,1,0:T(8,128)} %copy-done.3, ...), kind=kLoop, calls=%fused_computation.11 | loop fusion | flops 5474304 | bytes 5971968 | tf_op jit(solution)/shard_map/add | solution.py:36
  25.7 15.4 %all-gather.6.cloned.1.call-done = f32[4,3,3,6,4608]{4,3,2,1,0:T(8,128)} async-done(((f32[2,3,3,6,4608]{4,3,2,1,0:T(8,128)}), f32[4,3,3,6,4608]{4,3,2,1,0:T(8,128)}) %all-gather.6.cloned.1.call-update) | async-done | bytes 3981328 | tf_op jit(solution)/shard_map/all_gather | solution.py:9
  41.0 2.1 %broadcast_multiply_fusion.5 = (f32[3,6,4608]{2,1,0:T(8,128)S(1)}, f32[3,6,4608]{2,1,0:T(8,128)S(1)}, f32[3,6,4608]{2,1,0:T(8,128)S(1)}, f32[3,6,4608]{2,1,0:T(8...) fusion(f32[2,2,3,3,6,4608]{5,4,3,2,1,0:T(8,128)} %bitcast.118), kind=kLoop, calls=%fused_computation.72 | loop fusion | flops 497664 | bytes 3981312 | tf_op jit(solution)/shard_map/while/body/eval_jaxpr/mul | solution.py:32
  43.1 1.2 copy-done
  44.3 0.2 slice_bitcast_fusion.19
  44.5 0.9 subtract_add_fusion.2
  45.4 0.2 stack_broadcast_in_dim.2
  45.5 0.3 maximum_select_fusion
  45.9 0.2 slice_bitcast_fusion.1
  46.3 1.0 subtract_add_fusion
  47.2 0.8 fusion.8
  48.1 19.6 %all-reduce.3.cloned.1.call-done = f32[2,6,4608]{2,1,0:T(8,128)} async-done(((f32[2,6,4608]{2,1,0:T(8,128)}), f32[2,6,4608]{2,1,0:T(8,128)}) %all-reduce.3.cloned.1.call-update) | async-done | bytes 221200 | tf_op jit(solution)/shard_map/psum | solution.py:21
  67.7 0.9 dynamic-slice_bitcast_fusion
  68.6 0.7 copy.52
  69.3 61.6 %all-gather.4.cloned.1.call-done = f32[96,2,2304]{2,1,0:T(2,128)} async-done(((f32[6,2,2304]{2,1,0:T(2,128)}), f32[96,2,2304]{2,1,0:T(2,128)}) %all-gather.4.cloned.1.call-update) | async-done | bytes 1769488 | tf_op jit(solution)/shard_map/all_gather | solution.py:88
  131.0 2.9 %fusion.2 = f32[6,96]{1,0:T(8,128)S(1)} fusion(f32[6,2,2304]{2,0,1:T(8,128)S(1)} %dynamic-slice_bitcast_fusion, f32[96,2,2304]{2,1,0:T(2,128)} %all-gather.4.cloned.1.call-done), kind=kOutput, calls=%fused_computation.18 | convolution fusion | flops 31850496 | bytes 1882368 | tf_op jit(solution)/shard_map/dot_general | solution.py:47
  133.9 0.1 select_reduce_fusion
  134.1 2.5 %psum.15 = f32[6,49]{1,0:T(8,128)S(1)} all-reduce(f32[6,49]{1,0:T(8,128)S(1)} %select_reduce_fusion), channel_id=1, replica_groups=mesh['ta'=2,'gx'=16] {'ta'}, use_global_device_ids=true, to_apply=%region_2.3 | all-reduce | flops 294 | bytes 2352 | tf_op jit(solution)/shard_map/psum | solution.py:93
  136.5 0.6 broadcast_multiply_fusion.6
  (26 shorter events, 1.4 us)
Async XLA Ops:
  7.2 33.9 %all-gather.6.cloned.1.call-start = ((), (), s32[]{:S(2)}) async-start(), calls=%async_computation.2 | async-start | bytes 7962624 | tf_op jit(solution)/shard_map/all_gather | solution.py:9
  18.8 0.8 copy-start.1
  18.9 0.8 copy-start.2
  18.9 1.0 copy-start.3
  19.0 1.1 copy-start.4
  22.8 44.8 %all-reduce.3.cloned.1.call-start = ((), (), s32[]{:S(2)}) async-start(), calls=%async_computation | async-start | bytes 589824 | tf_op jit(solution)/shard_map/psum | solution.py:21
  41.0 3.3 %copy-start = (f32[4,3,3,6,4608]{4,3,2,1,0:T(8,128)S(1)}, f32[4,3,3,6,4608]{4,3,2,1,0:T(8,128)}, u32[]{:S(2)}) copy-start(f32[4,3,3,6,4608]{4,3,2,1,0:T(8,128)} %all-gather.6.cloned.1.call-done) | copy-start | bytes 11943940
  48.0 82.9 %all-gather.4.cloned.1.call-start = ((), (), s32[]{:S(2)}) async-start(), calls=%async_computation.1 | async-start | bytes 1880064 | tf_op jit(solution)/shard_map/all_gather | solution.py:88
Sparse Core Ops, SparseCore 0:
  22.9 18.0 all-gather.5
  48.2 19.4 all-reduce.2
  71.0 59.8 all-gather.3
where the time goes:
time: 144 us
  waiting for transfers between devices  96.6 us (67%)
  local copies, waits for them, and re-layouts  15.5 us (11%)
  between operations  14 us (10%)
  other arithmetic  11.8 us (8%)
  matrix products  2.94 us (2%)
  blocking collectives  2.47 us (2%)
    all_gather x1, waiting for transfers between devices, per_device(): shard_rows = lax.all_gather(loop_planes, 'gx', axis=0, tiled=True)  61.6 us
    psum x1, waiting for transfers between devices, spread(): return lax.psum(kept, axis)  19.6 us
    all_gather x1, waiting for transfers between devices, prefix(): pieces = lax.all_gather(value, axis)  15.4 us
    add x5, other arithmetic, complex_mul(): terms_real[0] + terms_real[1] + terms_real[2]  6.09 us
    slice x1, local copies, waits for them, and re-layouts, complex_mul(): right_real = right[0][middle:middle + 1]  5.72 us
    slice x2, local copies, waits for them, and re-layouts, complex_mul(): left_real = left[0][:, middle:middle + 1]  3.92 us
    dot_general x1, matrix products, correlation(): lax.dot_general(own_rows, others, (((1,), (1,)), ((), ())), precision=lax...  2.94 us
  transfers between devices with their start and end apart: 3, of which 3 were waited for; matrix products, arithmetic and copies ran while one was open for 2% of the time, Pallas kernels for 0%

commit v1 on v0

--- a/solution.py
+++ b/solution.py
@@ -2,6 +2,11 @@
 import jax.numpy as jnp
 from jax import lax
 from jax.sharding import PartitionSpec as P
+
+
+def begin_loads(x_local, a_name):
+    x_now = lax.all_gather(x_local, axis_name=a_name)
+    return jnp.sum(x_now, 0)
 
 
 def prefix(value, axis, join, neutral):
@@ -18,7 +23,7 @@
 
 def spread(value, axis, source):
     kept = jnp.where(lax.axis_index(axis) == source, value, 0).astype(value.dtype)
-    return lax.psum(kept, axis)
+    return begin_loads(kept, axis)
 
 
 def complex_mul(left, right):

time: 144 us -> 126 us (0.88)
  waiting for transfers between devices: 96.6 us -> 68.4 us
  local copies, waits for them, and re-layouts: 15.5 us -> 20.6 us
  other arithmetic: 11.8 us -> 14.6 us
  blocking collectives: 2.47 us -> 4.6 us
    psum x1 -> x0, waiting for transfers between devices: 19.6 us -> none  [spread(): return lax.psum(kept, axis)]
    all_gather x1, waiting for transfers between devices: 15.4 us -> 8.38 us  [prefix(): pieces = lax.all_gather(value, axis)]
    mul x15 -> x21, local copies, waits for them, and re-layouts: 1.6 us -> 7.12 us  [complex_mul(): terms_real.append(left_real * right_real - left_imag * right_imag)]
    add x5, other arithmetic: 6.09 us -> 8.55 us  [complex_mul(): terms_real[0] + terms_real[1] + terms_real[2]]
    all_gather x0 -> x1, blocking collectives: none -> 2.12 us  [begin_loads(): x_now = lax.all_gather(x_local, axis_name=a_name)]
    all_gather x1, waiting for transfers between devices: 61.6 us -> 60 us  [per_device(): shard_rows = lax.all_gather(loop_planes, 'gx', axis=0, tiled=True)]
  transfers between devices with their start and end apart: 3 -> 2, of which waited for: 3 -> 2; matrix products, arithmetic and copies ran while one was open for 2% -> 8% of each run, Pallas kernels for 0% -> 0%
where the time goes in v1:
time: 126 us
  waiting for transfers between devices  68.4 us (54%)
  local copies, waits for them, and re-layouts  20.6 us (16%)
  other arithmetic  14.6 us (12%)
  between operations  14.4 us (11%)
  blocking collectives  4.6 us (4%)
  matrix products  2.94 us (2%)
    all_gather x1, waiting for transfers between devices, per_device(): shard_rows = lax.all_gather(loop_planes, 'gx', axis=0, tiled=True)  60 us
    add x5, other arithmetic, complex_mul(): terms_real[0] + terms_real[1] + terms_real[2]  8.55 us
    all_gather x1, waiting for transfers between devices, prefix(): pieces = lax.all_gather(value, axis)  8.38 us
    mul x21, local copies, waits for them, and re-layouts, complex_mul(): terms_real.append(left_real * right_real - left_imag * right_imag)  7.12 us
    slice x1, local copies, waits for them, and re-layouts, complex_mul(): right_real = right[0][middle:middle + 1]  5.72 us
    slice x2, local copies, waits for them, and re-layouts, complex_mul(): left_real = left[0][:, middle:middle + 1]  3.92 us
    dot_general x1, matrix products, correlation(): lax.dot_general(own_rows, others, (((1,), (1,)), ((), ())), precision=lax...  2.94 us
    unnamed x20, local copies, waits for them, and re-layouts  2.68 us
  transfers between devices with their start and end apart: 2, of which 2 were waited for; matrix products, arithmetic and copies ran while one was open for 8% of the time, Pallas kernels for 0%

profile of v1, /device:TPU:0, one launch (start us, length us, event | category | flops | bytes accessed | tf_op | source)
XLA Modules:
  0.0 125.8 jit_solution(3021290334226141167)
XLA Ops:
  7.2 5.7 %fusion.10 = (f32[1,1,1,3,6,4608]{5,1,4,3,2,0:T(1,128)S(1)}, f32[1,1,1,3,6,4608]{5,1,4,3,2,0:T(1,128)S(1)}, f32[1,1,1,3,6,4608]{5,1,4,3,2,0:T(1,128)S(1)}, f32[1...) fusion(f32[3,2,3,3,6,4608]{5,1,4,3,2,0:T(2,128)} %param.1), kind=kLoop, calls=%fused_computation.87 | loop fusion | bytes 7962624 | tf_op jit(solution)/shard_map/slice | solution.py:35
  12.9 3.9 %fusion.11 = (f32[1,1,3,3,6,4608]{5,1,4,3,2,0:T(1,128)S(1)}, f32[1,1,3,3,6,4608]{5,1,4,3,2,0:T(1,128)S(1)}) fusion(f32[3,2,3,3,6,4608]{5,1,4,3,2,0:T(2,128)} %param.1), kind=kLoop, calls=%fused_computation.88 | loop fusion | bytes 3981312 | tf_op jit(solution)/shard_map/slice | solution.py:33
  16.9 0.3 copy_bitcast_fusion
  17.8 1.0 subtract_add_fusion.4
  19.3 0.3 copy-done.1
  20.1 0.9 subtract_add_fusion.3
  21.0 1.8 %pad_maximum_fusion = f32[2,3,3,6,4608]{4,3,2,1,0:T(8,128)} fusion(f32[1,3,3,6,4608]{4,3,2,1,0:T(8,128)S(1)} %get-tuple-element.60, f32[1,3,3,6,4608]{4,3,2,1,0:T(8,128)S(1)} %get-tuple-element.59), kind=kLoop, calls=%fused_computation | loop fusion | flops 497664 | bytes 3981312 | tf_op jit(solution)/shard_map/stack | solution.py:39
  22.8 0.2 all-gather.5.cloned.1.call-start
  23.1 1.0 copy.110
  24.1 1.0 copy.109
  25.1 1.0 copy.108
  26.1 1.0 copy.107
  27.1 1.0 copy.106
  28.1 0.2 copy.105
  28.4 3.8 %subtract_add_fusion.1 = (f32[3,3,6,4608]{3,1,2,0:T(4,128)S(1)}, f32[3,3,6,4608]{3,1,2,0:T(4,128)S(1)}) fusion(f32[3,6,4608]{2,0,1:T(4,128)} %copy.110, f32[3,6,4608]{2,1,0:T(8,128)S(1)} %get-tuple-element.81, f32[3,6,4608]{2,0,1:T(4,128)} %copy.109, f32[3,6,4608]{2,1,0:T(8,128)S(1)} %copy-done.6, f32[3,6,4608]{2,0,1:T(4,128)} %copy.108, ...), kind=kLoop, calls=%fused_computation.11 | loop fusion | flops 5474304 | bytes 5971968 | tf_op jit(solution)/shard_map/add | solution.py:41
  32.1 0.2 slice_bitcast_fusion.10
  32.4 0.2 slice_bitcast_fusion.12
  32.6 8.4 %all-gather.7.cloned.1.call-done = f32[4,3,3,6,4608]{4,3,2,1,0:T(8,128)} async-done(((f32[2,3,3,6,4608]{4,3,2,1,0:T(8,128)}), f32[4,3,3,6,4608]{4,3,2,1,0:T(8,128)}) %all-gather.7.cloned.1.call-update) | async-done | bytes 3981328 | tf_op jit(solution)/shard_map/all_gather | solution.py:14
  41.0 2.1 %broadcast_multiply_fusion.5 = (f32[3,6,4608]{2,1,0:T(8,128)S(1)}, f32[3,6,4608]{2,1,0:T(8,128)S(1)}, f32[3,6,4608]{2,1,0:T(8,128)S(1)}, f32[3,6,4608]{2,1,0:T(8...) fusion(f32[2,2,3,3,6,4608]{5,4,3,2,1,0:T(8,128)} %bitcast.119), kind=kLoop, calls=%fused_computation.70 | loop fusion | flops 497664 | bytes 3981312 | tf_op jit(solution)/shard_map/while/body/eval_jaxpr/mul | solution.py:37
  43.1 1.2 copy-done
  44.5 0.9 subtract_add_fusion.2
  45.5 0.3 maximum_select_fusion
  46.3 2.0 %subtract_add_fusion = (f32[1,3,3,6,4608]{4,2,3,1,0:T(4,128)S(1)}, f32[1,3,3,6,4608]{4,2,3,1,0:T(4,128)S(1)}) fusion(f32[3,6,4608]{2,0,1:T(4,128)S(1)} %get-tuple-element.75, f32[3,6,4608]{2,1,0:T(8,128)S(1)} %get-tuple-element.72, f32[3,6,4608]{2,0,1:T(4,128)S(1)} %get-tuple-element.69, f32[3,6,4608]{2,1,0:T(8,128)S(1)} %get-tuple-element.66, ...), kind=kLoop, calls=%fused_computation.9 | loop fusion | flops 5474304 | bytes 5971968 | tf_op jit(solution)/shard_map/add | solution.py:41
  48.3 0.7 broadcast_select_fusion
  49.0 2.1 %all-gather.1 = f32[4,1,1,6,4608]{4,2,3,1,0:T(1,128)S(1)} all-gather(f32[2,1,1,6,4608]{4,2,3,1,0:T(1,128)S(1)} %broadcast_select_fusion), channel_id=3, replica_groups=mesh['ta'=2,'gx'=16] {'ta'}, dimensions={0}, use_global_device_ids=true | all-gather | bytes 663552 | tf_op jit(solution)/shard_map/all_gather | solution.py:8
  51.3 0.3 reshape.307
  51.6 0.3 reduce_sum.18
  52.0 0.7 copy.115
  52.8 60.0 %all-gather.5.cloned.1.call-done = f32[96,2,2304]{2,1,0:T(2,128)} async-done(((f32[6,2,2304]{2,1,0:T(2,128)}), f32[96,2,2304]{2,1,0:T(2,128)}) %all-gather.5.cloned.1.call-update) | async-done | bytes 1769488 | tf_op jit(solution)/shard_map/all_gather | solution.py:93
  112.8 2.9 %fusion.2 = f32[6,96]{1,0:T(8,128)S(1)} fusion(f32[96,2,2304]{2,1,0:T(2,128)} %all-gather.5.cloned.1.call-done, f32[2,6,2304]{2,0,1:T(2,128)S(1)} %constant_dynamic-slice_fusion), kind=kOutput, calls=%fused_computation.18 | convolution fusion | flops 31850496 | bytes 1882368 | tf_op jit(solution)/shard_map/dot_general | solution.py:52
  115.8 2.5 %psum.7 = f32[6,49]{1,0:T(8,128)S(1)} all-reduce(f32[6,49]{1,0:T(8,128)S(1)} %select_reduce_fusion), channel_id=1, replica_groups=mesh['ta'=2,'gx'=16] {'ta'}, use_global_device_ids=true, to_apply=%region_2.3 | all-reduce | flops 294 | bytes 2352 | tf_op jit(solution)/shard_map/psum | solution.py:98
  118.3 0.6 broadcast_multiply_fusion.6
  (42 shorter events, 2.6 us)
Async XLA Ops:
  7.2 33.8 %all-gather.7.cloned.1.call-start = ((), (), s32[]{:S(2)}) async-start(), calls=%async_computation.1 | async-start | bytes 7962624 | tf_op jit(solution)/shard_map/all_gather | solution.py:14
  18.8 0.8 copy-start.1
  18.9 0.8 copy-start.3
  18.9 1.0 copy-start.5
  19.0 1.1 copy-start.7
  22.8 89.9 %all-gather.5.cloned.1.call-start = ((), (), s32[]{:S(2)}) async-start(), calls=%async_computation | async-start | bytes 1880064 | tf_op jit(solution)/shard_map/all_gather | solution.py:93
  26.1 2.3 %copy-start.2 = (f32[3,6,4608]{2,1,0:T(8,128)S(1)}, f32[3,6,4608]{2,1,0:T(8,128)}, u32[]{:S(2)}) copy-start(f32[3,6,4608]{2,1,0:T(8,128)} %copy-done.1) | copy-start | bytes 995332
  26.1 2.3 %copy-start.4 = (f32[3,6,4608]{2,1,0:T(8,128)S(1)}, f32[3,6,4608]{2,1,0:T(8,128)}, u32[]{:S(2)}) copy-start(f32[3,6,4608]{2,1,0:T(8,128)} %copy-done.3) | copy-start | bytes 995332
  26.1 2.3 %copy-start.6 = (f32[3,6,4608]{2,1,0:T(8,128)S(1)}, f32[3,6,4608]{2,1,0:T(8,128)}, u32[]{:S(2)}) copy-start(f32[3,6,4608]{2,1,0:T(8,128)} %copy-done.5) | copy-start | bytes 995332
  27.1 1.3 %copy-start.8 = (f32[3,6,4608]{2,1,0:T(8,128)S(1)}, f32[3,6,4608]{2,1,0:T(8,128)}, u32[]{:S(2)}) copy-start(f32[3,6,4608]{2,1,0:T(8,128)} %copy-done.7) | copy-start | bytes 995332
  41.0 3.3 %copy-start = (f32[4,3,3,6,4608]{4,3,2,1,0:T(8,128)S(1)}, f32[4,3,3,6,4608]{4,3,2,1,0:T(8,128)}, u32[]{:S(2)}) copy-start(f32[4,3,3,6,4608]{4,3,2,1,0:T(8,128)} %all-gather.7.cloned.1.call-done) | copy-start | bytes 11943940
Sparse Core Ops, SparseCore 0:
  22.9 18.0 all-gather.6
  52.8 59.8 all-gather.4
